TPU v7x, 8 devices: a whole 2x2x1 slice. The times are simulated.
8 devices in a mesh: dp: 1 (over z), cz: 2 (over y), cy: 2 (over x), cx: 2 (over core).
Axes of the slice: x: 2, y: 2, z: 1, core: 2. Of those that a mesh axis runs over, the one named last changes fastest.
Arguments:
- x_tokens: bfloat16 [4096, 2048], P(('dp', 'cx', 'cz'), 'cy')
- w_up: bfloat16 [2048, 16384], P('cy', ('cz', 'cx'))
- w_down: bfloat16 [16384, 2048], P('cz', ('cy', 'cx'))
Outputs:
- output: bfloat16 [4096, 2048], P(('dp', 'cx', 'cz'), 'cy')
All inputs are finite; a program needn't handle non-finite values.
Results may differ from a plain program's by a relative error of at most 0.0114676.
Values are sent between devices in bfloat16 or wider.
A program may use at most 1 GiB of HBM per device.

v0:
```python
import jax
import jax.numpy as jnp
from jax import lax
from jax.sharding import PartitionSpec as P, NamedSharding


def solution(mesh):
    data_spec = P(('dp', 'cx', 'cz'), 'cy')
    up_spec = P('cy', ('cz', 'cx'))
    down_spec = P('cz', ('cy', 'cx'))

    def local_mlp(x_local, w_up_local, w_down_local):
        x_block = lax.all_gather(x_local, 'cz', axis=0, tiled=True)
        w_up_block = lax.all_gather(w_up_local, 'cx', axis=1, tiled=True)
        partial_up = jnp.dot(x_block, w_up_block, preferred_element_type=jnp.float32)
        pre_act = lax.psum_scatter(partial_up, 'cy', scatter_dimension=0, tiled=True)
        hidden = jax.nn.gelu(pre_act.astype(jnp.bfloat16).astype(jnp.float32), approximate=True).astype(jnp.bfloat16)
        hidden_block = lax.all_gather(hidden, 'cy', axis=0, tiled=True)
        w_down_block = lax.all_gather(w_down_local, 'cx', axis=1, tiled=True)
        partial_down = jnp.dot(hidden_block, w_down_block, preferred_element_type=jnp.float32)
        out_local = lax.psum_scatter(partial_down, 'cz', scatter_dimension=0, tiled=True)
        return out_local.astype(jnp.bfloat16)

    return jax.shard_map(local_mlp, mesh=mesh, in_specs=(data_spec, up_spec, down_spec), out_specs=data_spec, check_vma=False)
```

profile of v0, /device:TPU:0, one launch (start us, length us, event | category | flops | bytes accessed | tf_op | source)
XLA Modules:
  0.0 1435.0 jit_solution(14928692666173003062)
XLA Ops:
  6.5 0.0 all-gather.5.cloned.1.call-start
  6.5 0.7 all-gather.5.cloned.1.call-update
  7.3 0.0 all-gather.7.cloned.1.call-start
  7.3 0.7 all-gather.7.cloned.1.call-update
  8.0 0.0 reduce-scatter.3.cloned.1.call-start
  8.1 57.8 %all-gather.5.cloned.1.call-done = bf16[2048,1024]{1,0:T(8,128)(2,1)} async-done(((bf16[1024,1024]{1,0:T(8,128)(2,1)}), bf16[2048,1024]{1,0:T(8,128)(2,1)}) %all-gather.5.cloned.1.call-update) | async-done | bytes 4194320 | tf_op jit(solution)/shard_map/all_gather | solution.py:13
  65.9 29.4 %all-gather.7.cloned.1.call-done = bf16[1024,8192]{1,0:T(8,128)(2,1)} async-done(((bf16[1024,4096]{1,0:T(8,128)(2,1)}), bf16[1024,8192]{1,0:T(8,128)(2,1)}) %all-gather.7.cloned.1.call-update) | async-done | bytes 16777232 | tf_op jit(solution)/shard_map/all_gather | solution.py:14
  95.3 44.8 %fusion.6 = f32[2048,8192]{1,0:T(8,128)} fusion(bf16[2048,1024]{1,0:T(8,128)(2,1)} %all-gather.5.cloned.1.call-done, bf16[1024,8192]{1,0:T(8,128)(2,1)} %all-gather.7.cloned.1.call-done), kind=kOutput, calls=%fused_computation.10 | convolution fusion | flops 34359738368 | bytes 88080384 | tf_op jit(solution)/shard_map/dot_general | solution.py:15
  140.0 0.0 reduce-scatter.3.cloned.1.call-update
  140.1 0.0 all-gather.11.cloned.1.call-start
  140.1 0.5 all-gather.11.cloned.1.call-update
  140.6 0.0 all-gather.9.cloned.1.call-start
  140.7 726.3 %reduce-scatter.3.cloned.1.call-done = f32[1024,8192]{1,0:T(8,128)} async-done(((f32[2048,8192]{1,0:T(8,128)}), f32[1024,8192]{1,0:T(8,128)}) %reduce-scatter.3.cloned.1.call-update) | async-done | bytes 33554448 | tf_op jit(solution)/shard_map/reduce_scatter | solution.py:16
  867.0 21.1 %fusion.5 = bf16[1024,8192]{1,0:T(8,128)(2,1)} fusion(f32[1024,8192]{1,0:T(8,128)} %reduce-scatter.3.cloned.1.call-done), kind=kLoop, calls=%fused_computation.9 | loop fusion | flops 92274688 | bytes 50331648 | tf_op jit(solution)/shard_map/convert_element_type | solution.py:17
  888.1 0.0 all-gather.9.cloned.1.call-update
  888.1 0.2 reduce-scatter.5.cloned.1.call-start
  888.3 7.9 all-gather.11.cloned.1.call-done
  896.2 388.1 %all-gather.9.cloned.1.call-done = bf16[2048,8192]{1,0:T(8,128)(2,1)} async-done(((bf16[1024,8192]{1,0:T(8,128)(2,1)}), bf16[2048,8192]{1,0:T(8,128)(2,1)}) %all-gather.9.cloned.1.call-update) | async-done | bytes 33554448 | tf_op jit(solution)/shard_map/all_gather | solution.py:18
  1284.3 43.4 %fusion.7 = f32[2048,1024]{1,0:T(8,128)} fusion(bf16[2048,8192]{1,0:T(8,128)(2,1)} %all-gather.9.cloned.1.call-done, bf16[8192,1024]{1,0:T(8,128)(2,1)} %all-gather.11.cloned.1.call-done), kind=kOutput, calls=%fused_computation.11 | convolution fusion | flops 34359738368 | bytes 58720256 | tf_op jit(solution)/shard_map/dot_general | solution.py:20
  1327.7 0.0 reduce-scatter.5.cloned.1.call-update
  1327.7 96.6 %reduce-scatter.5.cloned.1.call-done = f32[1024,1024]{1,0:T(8,128)} async-done(((f32[2048,1024]{1,0:T(8,128)}), f32[1024,1024]{1,0:T(8,128)}) %reduce-scatter.5.cloned.1.call-update) | async-done | bytes 4194320 | tf_op jit(solution)/shard_map/reduce_scatter | solution.py:21
  1424.3 3.8 convert_element_type.15
Async XLA Ops:
  6.5 59.4 %all-gather.5.cloned.1.call-start = ((), (), s32[]{:S(2)}) async-start(), calls=%async_computation.2 | async-start | bytes 6291456 | tf_op jit(solution)/shard_map/all_gather | solution.py:13
  7.3 88.0 %all-gather.7.cloned.1.call-start = ((), (), s32[]{:S(2)}) async-start(), calls=%async_computation.3 | async-start | bytes 25165824 | tf_op jit(solution)/shard_map/all_gather | solution.py:14
  8.0 859.0 %reduce-scatter.3.cloned.1.call-start = ((), (), s32[]{:S(2)}) async-start(), calls=%async_computation.4 | async-start | bytes 100663296 | tf_op jit(solution)/shard_map/reduce_scatter | solution.py:16
  140.1 756.2 %all-gather.11.cloned.1.call-start = ((), (), s32[]{:S(2)}) async-start(), calls=%async_computation.6 | async-start | bytes 25165824 | tf_op jit(solution)/shard_map/all_gather | solution.py:19
  140.6 1143.7 %all-gather.9.cloned.1.call-start = ((), (), s32[]{:S(2)}) async-start(), calls=%async_computation.5 | async-start | bytes 50331648 | tf_op jit(solution)/shard_map/all_gather | solution.py:18
  888.1 536.2 %reduce-scatter.5.cloned.1.call-start = ((), (), s32[]{:S(2)}) async-start(), calls=%async_computation.7 | async-start | bytes 12582912 | tf_op jit(solution)/shard_map/reduce_scatter | solution.py:21
Sparse Core Ops, SparseCore 0:
  8.8 57.0 all-gather.4
  67.4 27.8 all-gather.6
  140.2 726.7 reduce-scatter.2
  868.4 27.7 all-gather.10
  897.6 386.6 all-gather.8
  1327.9 96.4 reduce-scatter.4
where the time goes:
time: 1440 us
  waiting for transfers between devices  1310 us (91%)
  matrix products  88.2 us (6%)
  other arithmetic  24.9 us (2%)
    reduce_scatter x1, waiting for transfers between devices, local_mlp(): lax.psum_scatter(partial_up, 'cy', scatter_dimension=0, tiled=True)  726 us
    all_gather x1, waiting for transfers between devices, local_mlp(): hidden_block = lax.all_gather(hidden, 'cy', axis=0, tiled=True)  388 us
    reduce_scatter x1, waiting for transfers between devices, local_mlp(): lax.psum_scatter(partial_down, 'cz', scatter_dimension=0, tiled=True)  96.6 us
    all_gather x1, waiting for transfers between devices, local_mlp(): x_block = lax.all_gather(x_local, 'cz', axis=0, tiled=True)  57.8 us
    dot_general x1, matrix products, local_mlp(): jnp.dot(x_block, w_up_block, preferred_element_type=jnp.float32)  44.8 us
    dot_general x1, matrix products, local_mlp(): jnp.dot(hidden_block, w_down_block, preferred_element_type=jnp.float32)  43.4 us
    all_gather x1, waiting for transfers between devices, local_mlp(): w_up_block = lax.all_gather(w_up_local, 'cx', axis=1, tiled=True)  29.4 us
  transfers between devices with their start and end apart: 6, of which 6 were waited for; matrix products, arithmetic and copies ran while one was open for 1% of the time, Pallas kernels for 0%

commit v1 on v0

v1 whole, which is shorter than its diff:
```python
import jax
import jax.numpy as jnp
from jax import lax
from jax.sharding import PartitionSpec as P

SWAP = ((0, 1), (1, 0))
Z_CHUNKS = 4


def solution(mesh):
    data_spec = P(('dp', 'cx', 'cz'), 'cy')
    up_spec = P('cy', ('cz', 'cx'))
    down_spec = P('cz', ('cy', 'cx'))

    def local_mlp(x, w_up, w_down):
        cy = lax.axis_index('cy')
        half = w_up.shape[1] // 2
        xk = jnp.concatenate([x, lax.ppermute(x, 'cy', SWAP)], axis=1)
        x_other = lax.ppermute(xk, 'cz', SWAP)
        xs = jnp.concatenate([xk, x_other], axis=0)
        keep = lax.dynamic_slice_in_dim(w_up, cy * half, half, axis=1)
        send = lax.dynamic_slice_in_dim(w_up, (1 - cy) * half, half, axis=1)
        w1 = jnp.concatenate([keep, lax.ppermute(send, 'cy', SWAP)], axis=0)
        w1 = lax.all_gather(w1, 'cx', axis=1, tiled=True)
        pre = jnp.dot(xs, w1, preferred_element_type=jnp.float32).astype(jnp.bfloat16)
        h = jax.nn.gelu(pre.astype(jnp.float32), approximate=True).astype(jnp.bfloat16)
        w2v = w_down.reshape(2, 2, half, w_down.shape[1])
        w2k = lax.dynamic_index_in_dim(w2v, cy, axis=1, keepdims=False).reshape(2 * half, -1)
        w2s = lax.dynamic_index_in_dim(w2v, 1 - cy, axis=1, keepdims=False).reshape(2 * half, -1)
        w2r = lax.ppermute(w2s, 'cy', SWAP)
        w2_own = lax.all_gather(w2k, 'cx', axis=1, tiled=True)
        w2_oth = lax.all_gather(w2r, 'cx', axis=1, tiled=True)
        rows = x.shape[0]

        def over_z(w):
            z = jnp.dot(h, w, preferred_element_type=jnp.float32)
            return z[:rows] + lax.ppermute(z[rows:], 'cz', SWAP)

        n = w2_own.shape[1] // Z_CHUNKS
        own = [over_z(w2_own[:, c * n:(c + 1) * n]) for c in range(Z_CHUNKS)]
        oth = [over_z(w2_oth[:, c * n:(c + 1) * n]) for c in range(Z_CHUNKS)]
        out = [a + lax.ppermute(b, 'cy', SWAP) for a, b in zip(own, oth)]
        return jnp.concatenate(out, axis=1).astype(jnp.bfloat16)

    return jax.shard_map(local_mlp, mesh=mesh, in_specs=(data_spec, up_spec, down_spec), out_specs=data_spec, check_vma=False)
```

time: 1440 us -> 609 us (0.42)
  waiting for transfers between devices: 1310 us -> 371 us
  matrix products: 88.2 us -> 141 us
  local copies, waits for them, and re-layouts: 0 us -> 36.2 us
  starting transfers between devices: 0.38 us -> 20.7 us
    reduce_scatter x2 -> x0, waiting for transfers between devices: 823 us -> none  [the longest x1 726 us: local_mlp(): lax.psum_scatter(partial_up, 'cy', scatter_dimension=0, tiled=True)]
    all_gather x4 -> x3, waiting for transfers between devices: 483 us -> 0.01 us  [the longest x1 0.01 us: local_mlp(): w1 = lax.all_gather(w1, 'cx', axis=1, tiled=True)]
    ppermute x0 -> x16, waiting for transfers between devices: none -> 371 us  [the longest x1 90.6 us: local_mlp(): w1 = jnp.concatenate([keep, lax.ppermute(send, 'cy', SWAP)], axis=0)]
    dot_general x2 -> x9, matrix products: 88.2 us -> 141 us  [the longest x8 91.5 us: over_z(): z = jnp.dot(h, w, preferred_element_type=jnp.float32)]
    convert_element_type x2 -> x0, other arithmetic: 24.9 us -> none  [the longest x1 21.1 us: local_mlp(): jax.nn.gelu(pre_act.astype(jnp.bfloat16).astype(jnp.float32), approximate...]
    ppermute x0 -> x16, starting transfers between devices: none -> 20.1 us  [the longest x8 7.93 us: over_z(): return z[:rows] + lax.ppermute(z[rows:], 'cz', SWAP)]
    slice x0 -> x8, local copies, waits for them, and re-layouts: none -> 15.5 us  [over_z(): return z[:rows] + lax.ppermute(z[rows:], 'cz', SWAP)]
  transfers between devices with their start and end apart: 6 -> 19, of which waited for: 6 -> 11; matrix products, arithmetic and copies ran while one was open for 1% -> 30% of each run, Pallas kernels for 0% -> 0%
where the time goes in v1:
time: 609 us; the launch traced here: 606 us
  waiting for transfers between devices  371 us (61%)
  matrix products  141 us (23%)
  local copies, waits for them, and re-layouts  36.2 us (6%)
  other arithmetic  24.1 us (4%)
  starting transfers between devices  20.7 us (3%)
  between operations  13.9 us (2%)
    dot_general x8, matrix products, over_z(): z = jnp.dot(h, w, preferred_element_type=jnp.float32)  91.5 us
    ppermute x1, waiting for transfers between devices, local_mlp(): w1 = jnp.concatenate([keep, lax.ppermute(send, 'cy', SWAP)], axis=0)  90.6 us
    ppermute x1, waiting for transfers between devices, local_mlp(): w2r = lax.ppermute(w2s, 'cy', SWAP)  90 us
    ppermute x1, waiting for transfers between devices, local_mlp(): x_other = lax.ppermute(xk, 'cz', SWAP)  88.9 us
    dot_general x1, matrix products, local_mlp(): jnp.dot(xs, w1, preferred_element_type=jnp.float32).astype(jnp.bfloat16)  49.3 us
    ppermute x8, waiting for transfers between devices, over_z(): return z[:rows] + lax.ppermute(z[rows:], 'cz', SWAP)  47.1 us
    ppermute x1, waiting for transfers between devices, local_mlp(): xk = jnp.concatenate([x, lax.ppermute(x, 'cy', SWAP)], axis=1)  43.1 us
    slice x8, local copies, waits for them, and re-layouts, over_z(): return z[:rows] + lax.ppermute(z[rows:], 'cz', SWAP)  15.5 us
  transfers between devices with their start and end apart: 19, of which 11 were waited for; matrix products, arithmetic and copies ran while one was open for 30% of the time, Pallas kernels for 0%

profile of v1, /device:TPU:0, one launch (start us, length us, event | category | flops | bytes accessed | tf_op | source)
XLA Modules:
  0.0 606.4 jit_solution(754975577528957955)
XLA Ops:
  6.5 6.7 %constant_dynamic-slice_fusion.3 = (bf16[1024,2048]{1,0:T(8,128)(2,1)}, bf16[1024,2048]{1,0:T(8,128)(2,1)S(1)}) fusion(bf16[1024,4096]{1,0:T(8,128)(2,1)} %param.4, s32[]{:T(128)S(6)} %select_n.13, s32[]{:T(128)S(6)} %select_n.14), kind=kLoop, calls=%fused_computation.52 | loop fusion | bytes 16777224 | tf_op jit(solution)/shard_map/dynamic_slice | solution.py:21
  13.3 3.3 collective-permute-start.2
  16.6 90.6 %collective-permute-done.2 = bf16[1024,2048]{1,0:T(8,128)(2,1)S(1)} collective-permute-done((bf16[1024,2048]{1,0:T(8,128)(2,1)S(1)}, bf16[1024,2048]{1,0:T(8,128)(2,1)S(1)}, u32[]{:S(2)}, u32[]{:S(2)}) %collective-permute-start.2) | collective-permute-done | bytes 4194336 | tf_op jit(solution)/shard_map/ppermute | solution.py:23
  107.2 1.9 copy-done
  109.1 8.4 %pad_maximum_fusion = bf16[2048,2048]{1,0:T(8,128)(2,1)} fusion(bf16[1024,2048]{1,0:T(8,128)(2,1)} %copy-done, bf16[1024,2048]{1,0:T(8,128)(2,1)} %get-tuple-element.7), kind=kLoop, calls=%fused_computation.13 | loop fusion | flops 16777216 | bytes 16777216 | tf_op jit(solution)/shard_map/concatenate | solution.py:23
  117.5 0.0 all-gather.4.cloned.1.call-update
  117.5 0.0 all-gather.8.cloned.1.call-start
  117.6 6.5 %constant_dynamic-slice_fusion.1 = (bf16[2,1,2048,512]{3,2,1,0:T(8,128)(2,1)}, bf16[2,1,2048,512]{3,2,1,0:T(8,128)(2,1)S(1)}) fusion(bf16[2,2,2048,512]{3,2,1,0:T(8,128)(2,1)} %bitcast.13, s32[]{:T(128)S(6)} %select_n.15, s32[]{:T(128)S(6)} %select_n.16), kind=kLoop, calls=%fused_computation.50 | loop fusion | bytes 16777224 | tf_op jit(solution)/shard_map/jit(dynamic_index_in_dim)/dynamic_slice | solution.py:28
  124.1 1.7 collective-permute-start.4
  125.8 90.0 %collective-permute-done.4 = bf16[4096,512]{1,0:T(8,128)(2,1)} collective-permute-done((bf16[4096,512]{1,0:T(8,128)(2,1)S(1)}, bf16[4096,512]{1,0:T(8,128)(2,1)}, u32[]{:S(2)}, u32[]{:S(2)}) %collective-permute-start.4) | collective-permute-done | bytes 4194336 | tf_op jit(solution)/shard_map/ppermute | solution.py:30
  215.8 0.0 all-gather.8.cloned.1.call-update
  215.8 0.6 all-gather.6.cloned.1.call-start
  216.4 1.5 collective-permute-start
  217.9 1.5 constant_dynamic-update-slice_fusion.1
  219.4 43.1 %collective-permute-done = bf16[1024,1024]{1,0:T(8,128)(2,1)S(1)} collective-permute-done((bf16[1024,1024]{1,0:T(8,128)(2,1)S(1)}, bf16[1024,1024]{1,0:T(8,128)(2,1)S(1)}, u32[]{:S(2)}, u32[]{:S(2)}) %collective-permute-start) | collective-permute-done | bytes 2097184 | tf_op jit(solution)/shard_map/ppermute | solution.py:18
  262.5 1.5 constant_dynamic-update-slice_fusion
  264.0 1.2 collective-permute-start.1
  265.2 88.9 %collective-permute-done.1 = bf16[1024,2048]{1,0:T(8,128)(2,1)} collective-permute-done((bf16[1024,2048]{1,0:T(8,128)(2,1)}, bf16[1024,2048]{1,0:T(8,128)(2,1)}, u32[]{:S(2)}, u32[]{:S(2)}) %collective-permute-start.1) | collective-permute-done | bytes 4194336 | tf_op jit(solution)/shard_map/ppermute | solution.py:19
  354.1 49.3 %fusion.5 = bf16[2048,4096]{1,0:T(8,128)(2,1)} fusion(bf16[2048,4096]{1,0:T(8,128)(2,1)} %all-gather.4.cloned.1.call-done, bf16[1024,2048]{1,0:T(8,128)(2,1)} %collective-permute-done.1, bf16[1024,2048]{1,0:T(8,128)(2,1)} %constant_dynamic-update-slice_fusion), kind=kOutput, calls=%fused_computation.9 | convolution fusion | flops 34468790272 | bytes 41943040 | tf_op jit(solution)/shard_map/dot_general | solution.py:25
  403.4 8.9 %fusion.21 = f32[2048,256]{0,1:T(8,128)S(1)} fusion(bf16[2048,4096]{1,0:T(8,128)(2,1)} %fusion.5, bf16[4096,1024]{1,0:T(8,128)(2,1)} %all-gather.8.cloned.1.call-done), kind=kOutput, calls=%fused_computation.26 | convolution fusion | flops 4294967296 | bytes 20971520 | tf_op jit(solution)/shard_map/dot_general | solution.py:36
  412.4 1.2 slice.101
  413.5 0.9 collective-permute-start.5
  414.5 8.8 %fusion.23 = f32[2048,256]{0,1:T(8,128)S(1)} fusion(bf16[2048,4096]{1,0:T(8,128)(2,1)} %fusion.5, bf16[4096,1024]{1,0:T(8,128)(2,1)} %all-gather.6.cloned.1.call-done), kind=kOutput, calls=%fused_computation.28 | convolution fusion | flops 4294967296 | bytes 20971520 | tf_op jit(solution)/shard_map/dot_general | solution.py:36
  423.2 1.1 slice.98
  424.3 1.1 collective-permute-start.3
  425.4 12.3 %fusion.17 = f32[2048,256]{0,1:T(8,128)} fusion(bf16[2048,4096]{1,0:T(8,128)(2,1)} %fusion.5, bf16[4096,1024]{1,0:T(8,128)(2,1)} %all-gather.8.cloned.1.call-done), kind=kOutput, calls=%fused_computation.22 | convolution fusion | flops 4294967296 | bytes 20971520 | tf_op jit(solution)/shard_map/dot_general | solution.py:36
  437.7 2.3 slice.107
  440.0 0.9 collective-permute-start.8
  441.0 12.3 %fusion.13 = f32[2048,256]{0,1:T(8,128)} fusion(bf16[2048,4096]{1,0:T(8,128)(2,1)} %fusion.5, bf16[4096,1024]{1,0:T(8,128)(2,1)} %all-gather.8.cloned.1.call-done), kind=kOutput, calls=%fused_computation.18 | convolution fusion | flops 4294967296 | bytes 20971520 | tf_op jit(solution)/shard_map/dot_general | solution.py:36
  453.2 2.3 slice.113
  455.5 1.1 collective-permute-start.11
  456.6 12.5 %fusion.9 = f32[2048,256]{0,1:T(8,128)} fusion(bf16[2048,4096]{1,0:T(8,128)(2,1)} %fusion.5, bf16[4096,1024]{1,0:T(8,128)(2,1)} %all-gather.8.cloned.1.call-done), kind=kOutput, calls=%fused_computation.14 | convolution fusion | flops 4294967296 | bytes 20971520 | tf_op jit(solution)/shard_map/dot_general | solution.py:36
  469.1 2.3 slice.119
  471.4 0.9 collective-permute-start.14
  472.4 12.2 %fusion.19 = f32[2048,256]{0,1:T(8,128)} fusion(bf16[2048,4096]{1,0:T(8,128)(2,1)} %fusion.5, bf16[4096,1024]{1,0:T(8,128)(2,1)} %all-gather.6.cloned.1.call-done), kind=kOutput, calls=%fused_computation.24 | convolution fusion | flops 4294967296 | bytes 20971520 | tf_op jit(solution)/shard_map/dot_general | solution.py:36
  484.6 12.2 %fusion.15 = f32[2048,256]{0,1:T(8,128)} fusion(bf16[2048,4096]{1,0:T(8,128)(2,1)} %fusion.5, bf16[4096,1024]{1,0:T(8,128)(2,1)} %all-gather.6.cloned.1.call-done), kind=kOutput, calls=%fused_computation.20 | convolution fusion | flops 4294967296 | bytes 20971520 | tf_op jit(solution)/shard_map/dot_general | solution.py:36
  496.8 2.5 slice.104
  499.3 2.3 slice.110
  501.6 1.1 collective-permute-start.7
  502.7 2.7 slice_add_fusion.6
  505.4 0.9 collective-permute-start.10
  506.4 2.7 slice_add_fusion.4
  509.1 1.5 collective-permute-start.6
  510.6 2.3 slice_add_fusion.2
  512.9 0.5 collective-permute-start.9
  513.5 16.0 %collective-permute-done.14 = f32[1024,256]{0,1:T(8,128)} collective-permute-done((f32[1024,256]{0,1:T(8,128)}, f32[1024,256]{0,1:T(8,128)}, u32[]{:S(2)}, u32[]{:S(2)}) %collective-permute-start.14) | collective-permute-done | bytes 1048608 | tf_op jit(solution)/shard_map/ppermute | solution.py:37
  529.4 0.9 collective-permute-start.12
  530.6 12.3 %fusion.11 = f32[2048,256]{0,1:T(8,128)} fusion(bf16[2048,4096]{1,0:T(8,128)(2,1)} %fusion.5, bf16[4096,1024]{1,0:T(8,128)(2,1)} %all-gather.6.cloned.1.call-done), kind=kOutput, calls=%fused_computation.16 | convolution fusion | flops 4294967296 | bytes 20971520 | tf_op jit(solution)/shard_map/dot_general | solution.py:36
  542.9 1.5 slice.116
  544.3 2.4 slice_add_fusion
  546.7 5.2 collective-permute-done.7
  551.9 0.9 collective-permute-start.13
  552.9 1.5 collective-permute-start.15
  554.3 1.4 fusion.32
  555.8 1.8 collective-permute-done.9
  557.6 1.8 fusion.30
  559.4 15.0 %collective-permute-done.10 = f32[1024,256]{0,1:T(8,128)} collective-permute-done((f32[1024,256]{0,1:T(8,128)}, f32[1024,256]{0,1:T(8,128)}, u32[]{:S(2)}, u32[]{:S(2)}) %collective-permute-start.10) | collective-permute-done | bytes 1048608 | tf_op jit(solution)/shard_map/ppermute | solution.py:37
  574.4 5.7 collective-permute-done.12
  580.1 1.8 fusion.28
  581.9 10.9 %collective-permute-done.13 = f32[1024,256]{0,1:T(8,128)S(1)} collective-permute-done((f32[1024,256]{0,1:T(8,128)S(1)}, f32[1024,256]{0,1:T(8,128)S(1)}, u32[]{:S(2)}, u32[]{:S(2)}) %collective-permute-start.13) | collective-permute-done | bytes 1048608 | tf_op jit(solution)/shard_map/ppermute | solution.py:37
  592.8 3.5 collective-permute-done.15
  596.3 0.3 fusion.26
  596.7 0.2 pad_maximum_fusion.1
  596.9 2.6 copy.12
  (23 shorter events, 0.1 us)
Async XLA Ops:
  6.5 347.6 %all-gather.4.cloned.1.call-start = ((), (), s32[]{:S(2)}) async-start(), calls=%async_computation | async-start | bytes 25165824 | tf_op jit(solution)/shard_map/all_gather | solution.py:24
  13.3 93.9 %collective-permute-start.2 = (bf16[1024,2048]{1,0:T(8,128)(2,1)S(1)}, bf16[1024,2048]{1,0:T(8,128)(2,1)S(1)}, u32[]{:S(2)}, u32[]{:S(2)}) collective-permute-start(bf16[1024,2048]{1,0:T(8,128)(2,1)S(1)} %get-tuple-element.8), channel_id=1, source_target_pairs={{0,2},{2,0},{1,3},{3,1},{4,6},{6,4},{5,7},{7,5}} | collective-permute-start | bytes 12582920 | tf_op jit(solution)/shard_map/ppermute | solution.py:23
  107.2 1.9 copy-start
  117.5 285.9 %all-gather.8.cloned.1.call-start = ((), (), s32[]{:S(2)}) async-start(), calls=%async_computation.2 | async-start | bytes 12582912 | tf_op jit(solution)/shard_map/all_gather | solution.py:32
  117.6 98.8 %copy-start.6 = (bf16[1024,1024]{1,0:T(8,128)(2,1)S(1)}, bf16[1024,1024]{1,0:T(8,128)(2,1)}, u32[]{:S(2)}) copy-start(bf16[1024,1024]{1,0:T(8,128)(2,1)} %param.3) | copy-start | bytes 6291460
  124.1 91.7 %collective-permute-start.4 = (bf16[4096,512]{1,0:T(8,128)(2,1)S(1)}, bf16[4096,512]{1,0:T(8,128)(2,1)}, u32[]{:S(2)}, u32[]{:S(2)}) collective-permute-start(bf16[4096,512]{1,0:T(8,128)(2,1)S(1)} %bitcast.14), channel_id=1, source_target_pairs={{0,2},{2,0},{1,3},{3,1},{4,6},{6,4},{5,7},{7,5}} | collective-permute-start | bytes 12582920 | tf_op jit(solution)/shard_map/ppermute | solution.py:30
  215.8 198.6 %all-gather.6.cloned.1.call-start = ((), (), s32[]{:S(2)}) async-start(), calls=%async_computation.1 | async-start | bytes 12582912 | tf_op jit(solution)/shard_map/all_gather | solution.py:31
  216.4 46.1 %collective-permute-start = (bf16[1024,1024]{1,0:T(8,128)(2,1)S(1)}, bf16[1024,1024]{1,0:T(8,128)(2,1)S(1)}, u32[]{:S(2)}, u32[]{:S(2)}) collective-permute-start(bf16[1024,1024]{1,0:T(8,128)(2,1)S(1)} %copy-done.6), channel_id=1, source_target_pairs={{0,2},{2,0},{1,3},{3,1},{4,6},{6,4},{5,7},{7,5}} | collective-permute-start | bytes 6291464 | tf_op jit(solution)/shard_map/ppermute | solution.py:18
  264.0 90.1 %collective-permute-start.1 = (bf16[1024,2048]{1,0:T(8,128)(2,1)}, bf16[1024,2048]{1,0:T(8,128)(2,1)}, u32[]{:S(2)}, u32[]{:S(2)}) collective-permute-start(bf16[1024,2048]{1,0:T(8,128)(2,1)} %constant_dynamic-update-slice_fusion), channel_id=1, source_target_pairs={{0,4},{4,0},{1,5},{5,1},{2,6},{6,2},{3,7},{7,3}} | collective-permute-start | bytes 12582920 | tf_op jit(solution)/shard_map/ppermute | solution.py:19
  412.4 2.1 copy-start.4
  413.5 88.1 %collective-permute-start.5 = (f32[1024,256]{0,1:T(8,128)}, f32[1024,256]{0,1:T(8,128)}, u32[]{:S(2)}, u32[]{:S(2)}) collective-permute-start(f32[1024,256]{0,1:T(8,128)} %slice.101), channel_id=1, source_target_pairs={{0,4},{4,0},{1,5},{5,1},{2,6},{6,2},{3,7},{7,3}} | collective-permute-start | bytes 3145736 | tf_op jit(solution)/shard_map/ppermute | solution.py:37
  424.3 88.6 %collective-permute-start.3 = (f32[1024,256]{0,1:T(8,128)}, f32[1024,256]{0,1:T(8,128)S(1)}, u32[]{:S(2)}, u32[]{:S(2)}) collective-permute-start(f32[1024,256]{0,1:T(8,128)} %slice.98), channel_id=1, source_target_pairs={{0,4},{4,0},{1,5},{5,1},{2,6},{6,2},{3,7},{7,3}} | collective-permute-start | bytes 3145736 | tf_op jit(solution)/shard_map/ppermute | solution.py:37
  440.0 65.4 %collective-permute-start.8 = (f32[1024,256]{0,1:T(8,128)}, f32[1024,256]{0,1:T(8,128)}, u32[]{:S(2)}, u32[]{:S(2)}) collective-permute-start(f32[1024,256]{0,1:T(8,128)} %slice.107), channel_id=1, source_target_pairs={{0,4},{4,0},{1,5},{5,1},{2,6},{6,2},{3,7},{7,3}} | collective-permute-start | bytes 3145736 | tf_op jit(solution)/shard_map/ppermute | solution.py:37
  455.5 53.6 %collective-permute-start.11 = (f32[1024,256]{0,1:T(8,128)}, f32[1024,256]{0,1:T(8,128)}, u32[]{:S(2)}, u32[]{:S(2)}) collective-permute-start(f32[1024,256]{0,1:T(8,128)} %slice.113), channel_id=1, source_target_pairs={{0,4},{4,0},{1,5},{5,1},{2,6},{6,2},{3,7},{7,3}} | collective-permute-start | bytes 3145736 | tf_op jit(solution)/shard_map/ppermute | solution.py:37
  471.4 58.0 %collective-permute-start.14 = (f32[1024,256]{0,1:T(8,128)}, f32[1024,256]{0,1:T(8,128)}, u32[]{:S(2)}, u32[]{:S(2)}) collective-permute-start(f32[1024,256]{0,1:T(8,128)} %slice.119), channel_id=1, source_target_pairs={{0,4},{4,0},{1,5},{5,1},{2,6},{6,2},{3,7},{7,3}} | collective-permute-start | bytes 3145736 | tf_op jit(solution)/shard_map/ppermute | solution.py:37
  496.8 13.8 %copy-start.5 = (f32[2048,256]{0,1:T(8,128)S(1)}, f32[2048,256]{0,1:T(8,128)}, u32[]{:S(2)}) copy-start(f32[2048,256]{0,1:T(8,128)} %fusion.13) | copy-start | bytes 6291460
  501.6 50.3 %collective-permute-start.7 = (f32[1024,256]{0,1:T(8,128)}, f32[1024,256]{0,1:T(8,128)}, u32[]{:S(2)}, u32[]{:S(2)}) collective-permute-start(f32[1024,256]{0,1:T(8,128)} %slice.104), channel_id=1, source_target_pairs={{0,4},{4,0},{1,5},{5,1},{2,6},{6,2},{3,7},{7,3}} | collective-permute-start | bytes 3145736 | tf_op jit(solution)/shard_map/ppermute | solution.py:37
  505.4 69.0 %collective-permute-start.10 = (f32[1024,256]{0,1:T(8,128)}, f32[1024,256]{0,1:T(8,128)}, u32[]{:S(2)}, u32[]{:S(2)}) collective-permute-start(f32[1024,256]{0,1:T(8,128)} %slice.110), channel_id=1, source_target_pairs={{0,4},{4,0},{1,5},{5,1},{2,6},{6,2},{3,7},{7,3}} | collective-permute-start | bytes 3145736 | tf_op jit(solution)/shard_map/ppermute | solution.py:37
  509.1 43.7 %collective-permute-start.6 = (f32[1024,256]{0,1:T(8,128)}, f32[1024,256]{0,1:T(8,128)}, u32[]{:S(2)}, u32[]{:S(2)}) collective-permute-start(f32[1024,256]{0,1:T(8,128)} %slice_add_fusion.6), channel_id=1, source_target_pairs={{0,2},{2,0},{1,3},{3,1},{4,6},{6,4},{5,7},{7,5}} | collective-permute-start | bytes 3145736 | tf_op jit(solution)/shard_map/ppermute | solution.py:42
  512.9 44.7 %collective-permute-start.9 = (f32[1024,256]{0,1:T(8,128)}, f32[1024,256]{0,1:T(8,128)}, u32[]{:S(2)}, u32[]{:S(2)}) collective-permute-start(f32[1024,256]{0,1:T(8,128)} %slice_add_fusion.4), channel_id=1, source_target_pairs={{0,2},{2,0},{1,3},{3,1},{4,6},{6,4},{5,7},{7,5}} | collective-permute-start | bytes 3145736 | tf_op jit(solution)/shard_map/ppermute | solution.py:42
  529.4 50.6 %collective-permute-start.12 = (f32[1024,256]{0,1:T(8,128)}, f32[1024,256]{0,1:T(8,128)}, u32[]{:S(2)}, u32[]{:S(2)}) collective-permute-start(f32[1024,256]{0,1:T(8,128)} %slice_add_fusion.2), channel_id=1, source_target_pairs={{0,2},{2,0},{1,3},{3,1},{4,6},{6,4},{5,7},{7,5}} | collective-permute-start | bytes 3145736 | tf_op jit(solution)/shard_map/ppermute | solution.py:42
  542.9 14.8 %copy-start.2 = (f32[2048,256]{0,1:T(8,128)S(1)}, f32[2048,256]{0,1:T(8,128)}, u32[]{:S(2)}) copy-start(f32[2048,256]{0,1:T(8,128)} %fusion.19) | copy-start | bytes 6291460
  542.9 37.2 %copy-start.1 = (f32[2048,256]{0,1:T(8,128)S(1)}, f32[2048,256]{0,1:T(8,128)}, u32[]{:S(2)}) copy-start(f32[2048,256]{0,1:T(8,128)} %fusion.15) | copy-start | bytes 6291460
  542.9 53.5 %copy-start.3 = (f32[2048,256]{0,1:T(8,128)S(1)}, f32[2048,256]{0,1:T(8,128)}, u32[]{:S(2)}) copy-start(f32[2048,256]{0,1:T(8,128)} %fusion.11) | copy-start | bytes 6291460
  551.9 40.9 %collective-permute-start.13 = (f32[1024,256]{0,1:T(8,128)S(1)}, f32[1024,256]{0,1:T(8,128)S(1)}, u32[]{:S(2)}, u32[]{:S(2)}) collective-permute-start(f32[1024,256]{0,1:T(8,128)S(1)} %slice.116), channel_id=1, source_target_pairs={{0,4},{4,0},{1,5},{5,1},{2,6},{6,2},{3,7},{7,3}} | collective-permute-start | bytes 3145736 | tf_op jit(solution)/shard_map/ppermute | solution.py:37
  552.9 43.5 %collective-permute-start.15 = (f32[1024,256]{0,1:T(8,128)S(1)}, f32[1024,256]{0,1:T(8,128)S(1)}, u32[]{:S(2)}, u32[]{:S(2)}) collective-permute-start(f32[1024,256]{0,1:T(8,128)S(1)} %slice_add_fusion), channel_id=1, source_target_pairs={{0,2},{2,0},{1,3},{3,1},{4,6},{6,4},{5,7},{7,5}} | collective-permute-start | bytes 3145736 | tf_op jit(solution)/shard_map/ppermute | solution.py:42
Sparse Core Ops, SparseCore 0:
  117.7 29.0 all-gather.3
  216.0 18.9 all-gather.7
  265.4 18.0 all-gather.5

commit v2 on v0

v2 whole, which is shorter than its diff:
```python
import functools

import jax
import jax.numpy as jnp
from jax import lax
from jax.experimental import pallas as pl
from jax.experimental.pallas import tpu as pltpu
from jax.sharding import PartitionSpec as P

MESH = pl.DeviceIdType.MESH
F32, BF16 = jnp.float32, jnp.bfloat16
N1 = 8
N2 = 4
MT = 512
ORDER = ((0, 0), (0, 1), (1, 0), (1, 1), (1, 2), (1, 3), (0, 2), (0, 3))


def gelu(c):
    return c * (0.5 * (1.0 + jnp.tanh(0.7978845608028654 * (c + 0.044715 * (c * c * c)))))


def kernel(x, w1, w2, out, g0, g1, xg, w1g, h, w2s, ry, rx, zs, zo, ob,
           lsem, osem, xs, xr, ws, wr, vs, vr, ts, tr, ys, yr, zys, zyr,
           ds1, dr1, fs1, fr1, ds2, dr2, fs2, fr2):
    cz, cy, cx = lax.axis_index('cz'), lax.axis_index('cy'), lax.axis_index('cx')
    X, Y, D = {'cy': 1 - cy}, {'cz': 1 - cz}, {'cx': 1 - cx}
    R, K = x.shape
    HB = w1.shape[1] // 2
    WC = HB // N1
    LC = w2.shape[1] // N2

    def remote(src, dst, s, r, dev):
        return pltpu.make_async_remote_copy(src, dst, s, r, device_id=dev, device_id_type=MESH)

    barrier = pltpu.get_barrier_semaphore()
    for dev in (X, Y, D):
        pl.semaphore_signal(barrier, inc=1, device_id=dev, device_id_type=MESH)
    pl.semaphore_wait(barrier, 3)

    own, oth = pl.ds(0, R), pl.ds(R, R)
    mine = pl.multiple_of(cx * HB, HB)
    keep = pl.multiple_of(cy * HB, HB)
    give = pl.multiple_of((1 - cy) * HB, HB)

    x_x = remote(x, xg.at[own, pl.ds(K, K)], xs.at[0], xr.at[0], X)
    y_x = remote(x, xg.at[oth, pl.ds(0, K)], ys.at[0], yr.at[0], Y)
    y_xf = remote(xg.at[own, pl.ds(K, K)], xg.at[oth, pl.ds(K, K)], ys.at[1], yr.at[1], Y)
    l_x = pltpu.make_async_copy(x, xg.at[own, pl.ds(0, K)], lsem.at[0])
    l_w1 = pltpu.make_async_copy(w1.at[:, pl.ds(keep, HB)], w1g.at[pl.ds(0, K), pl.ds(mine, HB)], lsem.at[1])
    d_w1 = remote(w1.at[:, pl.ds(keep, HB)], w1g.at[pl.ds(0, K), pl.ds(mine, HB)], ds1.at[0], dr1.at[0], D)

    def x_w1(j):
        return remote(w1.at[:, pl.ds(pl.multiple_of(give + j * WC, WC), WC)],
                      w1g.at[pl.ds(K, K), pl.ds(pl.multiple_of(mine + j * WC, WC), WC)],
                      ws.at[j], wr.at[j], X)

    def f_w1(j):
        blk = w1g.at[pl.ds(K, K), pl.ds(pl.multiple_of(mine + j * WC, WC), WC)]
        return remote(blk, blk, fs1.at[j], fr1.at[j], D)

    lanes = pl.ds(pl.multiple_of(cx * LC, LC), LC)
    lanes_p = pl.ds(pl.multiple_of((1 - cx) * LC, LC), LC)

    def x_w2(c, b):
        return remote(w2.at[pl.ds(pl.multiple_of(b * 2 * HB + give, HB), HB), pl.ds(c * LC, LC)],
                      g1.at[c, pl.ds(b * HB, HB), lanes], vs.at[c * 2 + b], vr.at[c * 2 + b], X)

    def f_w2(c):
        blk = g1.at[c, :, lanes]
        return remote(blk, blk, fs2.at[c], fr2.at[c], D)

    def d_w2(c, b):
        return remote(w2.at[pl.ds(pl.multiple_of(b * 2 * HB + keep, HB), HB), pl.ds(c * LC, LC)],
                      g0.at[c, pl.ds(b * HB, HB), :], ds2.at[c * 2 + b], dr2.at[c * 2 + b], D)

    def loads(q):
        kind, c = ORDER[q]
        s = q % 2
        if kind == 1:
            return [pltpu.make_async_copy(g1.at[c], w2s.at[s], lsem.at[2 + 3 * s])]
        got = [pltpu.make_async_copy(g0.at[c], w2s.at[s, :, lanes_p], lsem.at[2 + 3 * s])]
        for b in range(2):
            got.append(pltpu.make_async_copy(
                w2.at[pl.ds(pl.multiple_of(b * 2 * HB + keep, HB), HB), pl.ds(c * LC, LC)],
                w2s.at[s, pl.ds(b * HB, HB), lanes], lsem.at[3 + 3 * s + b]))
        return got

    def z_y(q):
        return remote(zs.at[q % 2], ry.at[q], zys.at[q], zyr.at[q], Y)

    def z_x(c):
        q = ORDER.index((1, c))
        return remote(ry.at[q], rx.at[c], ts.at[c], tr.at[c], X)

    x_x.start()
    y_x.start()
    l_x.start()
    l_w1.start()
    for j in range(N1):
        x_w1(j).start()
    d_w1.start()
    for c in range(N2):
        for b in range(2):
            d_w2(c, b).start()

    def layer1(row0, rows, block, j):
        col = pl.ds(pl.multiple_of(block * HB + j * WC, WC), WC)

        @pl.loop(0, rows // MT)
        def _(i):
            r = pl.ds(pl.multiple_of(row0 + i * MT, MT), MT)
            c = jnp.dot(xg[r, :], w1g[:, col], preferred_element_type=F32)
            h[r, col] = gelu(c.astype(BF16).astype(F32)).astype(BF16)

    x_x.wait_recv()
    y_xf.start()
    l_x.wait()
    l_w1.wait()
    d_w1.wait_recv()

    def prepare(q):
        kind, c = ORDER[q]
        if kind == 1:
            x_w2(c, 0).wait_recv()
            x_w2(c, 1).wait_recv()
            f_w2(c).start()
            f_w2(c).wait_recv()
        else:
            d_w2(c, 0).wait_recv()
            d_w2(c, 1).wait_recv()
        for cp in loads(q):
            cp.start()

    @pl.loop(0, N1 // 2)
    def _(j):
        x_w1(j).wait_recv()
        f_w1(j).start()
        layer1(0, R, cx, j)
        f_w1(j).wait_recv()
        layer1(0, R, 1 - cx, j)

    y_x.wait_recv()
    y_xf.wait_recv()

    @pl.loop(0, N1 // 2)
    def _(j):
        layer1(R, R, cx, j)
        layer1(R, R, 1 - cx, j)

    prepare(0)
    prepare(1)
    for c in range(N2):
        for b in range(2):
            x_w2(c, b).start()

    @pl.loop(N1 // 2, N1)
    def _(j):
        x_w1(j).wait_recv()
        f_w1(j).start()
        layer1(0, 2 * R, cx, j)
        f_w1(j).wait_recv()
        layer1(0, 2 * R, 1 - cx, j)

    def layer2(dst, row0, s):
        @pl.loop(0, R // MT)
        def _(i):
            r = pl.multiple_of(i * MT, MT)
            dst[pl.ds(r, MT), :] = jnp.dot(h[pl.ds(row0 + r, MT), :], w2s[s], preferred_element_type=F32)

    def absorb(q):
        z_y(q).wait()
        ry[q] = ry[q] + zo[q % 2]
        kind, c = ORDER[q]
        if kind == 1:
            z_x(c).start()

    def stores(c):
        return [pltpu.make_async_copy(ob.at[c % 2, :, pl.ds(k * LC, LC)],
                                      out.at[:, pl.ds(k * N2 * LC + c * LC, LC)], osem.at[2 * c + k])
                for k in range(2)]

    def finish(c):
        z_x(c).wait_recv()
        if c >= 2:
            for cp in stores(c - 2):
                cp.wait()
        ob[c % 2] = (ry[ORDER.index((0, c))] + rx[c]).astype(BF16)
        for cp in stores(c):
            cp.start()

    last = len(ORDER) - 1
    for q in range(len(ORDER)):
        for cp in loads(q):
            cp.wait()
        layer2(zs.at[q % 2], R, q % 2)
        z_y(q).start()
        layer2(zo.at[q % 2], 0, q % 2)
        if q >= 1:
            absorb(q - 1)
        if q + 2 <= last:
            prepare(q + 2)
        if q == 5:
            finish(0)
        if q == 6:
            finish(1)
    finish(2)
    z_x(3).wait_recv()
    rx[3] = rx[3] + zo[last % 2]
    z_y(last).wait()
    for cp in stores(1):
        cp.wait()
    ob[1] = (ry[last] + rx[3]).astype(BF16)
    for cp in stores(3):
        cp.start()
    for c in (2, 3):
        for cp in stores(c):
            cp.wait()
    for cp in [x_x, y_x, y_xf, d_w1] + [z_x(c) for c in range(N2)] + [f_w2(c) for c in range(N2)]:
        cp.wait_send()
    for c in range(N2):
        for b in range(2):
            x_w2(c, b).wait_send()
            d_w2(c, b).wait_send()

    @pl.loop(0, N1)
    def _(j):
        x_w1(j).wait_send()
        f_w1(j).wait_send()


def solution(mesh):
    data_spec = P(('dp', 'cx', 'cz'), 'cy')
    up_spec = P('cy', ('cz', 'cx'))
    down_spec = P('cz', ('cy', 'cx'))

    def local_mlp(x, w1, w2):
        R, K = x.shape
        HB = w1.shape[1] // 2
        LC = w2.shape[1] // N2
        nq = len(ORDER)
        dma = pltpu.SemaphoreType.DMA
        any_spec = pl.BlockSpec(memory_space=pl.ANY)
        scratch = [
            pltpu.VMEM((2 * R, 2 * K), BF16),
            pltpu.VMEM((2 * K, 2 * HB), BF16),
            pltpu.VMEM((2 * R, 2 * HB), BF16),
            pltpu.VMEM((2, 2 * HB, 2 * LC), BF16),
            pltpu.VMEM((nq, R, 2 * LC), F32),
            pltpu.VMEM((N2, R, 2 * LC), F32),
            pltpu.VMEM((2, R, 2 * LC), F32),
            pltpu.VMEM((2, R, 2 * LC), F32),
            pltpu.VMEM((2, R, 2 * LC), BF16),
            dma((8,)), dma((8,)),
            dma((1,)), dma((1,)),
            dma((N1,)), dma((N1,)),
            dma((2 * N2,)), dma((2 * N2,)),
            dma((N2,)), dma((N2,)),
            dma((2,)), dma((2,)),
            dma((nq,)), dma((nq,)),
            dma((1,)), dma((1,)), dma((N1,)), dma((N1,)),
            dma((2 * N2,)), dma((2 * N2,)), dma((N2,)), dma((N2,)),
        ]
        z, _, _ = pl.pallas_call(
            kernel,
            out_shape=(jax.ShapeDtypeStruct((R, K), BF16),
                       jax.ShapeDtypeStruct((N2, 2 * HB, LC), BF16),
                       jax.ShapeDtypeStruct((N2, 2 * HB, 2 * LC), BF16)),
            in_specs=[any_spec] * 3,
            out_specs=(any_spec,) * 3,
            scratch_shapes=scratch,
            compiler_params=pltpu.CompilerParams(
                collective_id=0, has_side_effects=True, vmem_limit_bytes=67043328),
            name='mlp',
        )(x, w1, w2)
        return z

    return jax.shard_map(local_mlp, mesh=mesh, in_specs=(data_spec, up_spec, down_spec), out_specs=data_spec, check_vma=False)
```

time: 1440 us -> 335 us (0.23)
  waiting for transfers between devices: 1310 us -> 0 us
  Pallas kernels: 0 us -> 332 us
  matrix products: 88.2 us -> 0 us
  other arithmetic: 24.9 us -> 0 us
    reduce_scatter x2 -> x0, waiting for transfers between devices: 823 us -> none  [the longest x1 726 us: local_mlp(): lax.psum_scatter(partial_up, 'cy', scatter_dimension=0, tiled=True)]
    all_gather x4 -> x0, waiting for transfers between devices: 483 us -> none  [the longest x1 388 us: local_mlp(): hidden_block = lax.all_gather(hidden, 'cy', axis=0, tiled=True)]
    pallas_call x0 -> x1, Pallas kernels: none -> 332 us  [local_mlp(): pl.pallas_call(kernel, out_shape=(jax.ShapeDtypeStruct((R, K), BF16), jax...]
    dot_general x2 -> x0, matrix products: 88.2 us -> none  [the longest x1 44.8 us: local_mlp(): jnp.dot(x_block, w_up_block, preferred_element_type=jnp.float32)]
    convert_element_type x2 -> x0, other arithmetic: 24.9 us -> none  [the longest x1 21.1 us: local_mlp(): jax.nn.gelu(pre_act.astype(jnp.bfloat16).astype(jnp.float32), approximate...]
  transfers between devices with their start and end apart: 6 -> 0, of which waited for: 6 -> 0; matrix products, arithmetic and copies ran while one was open for 1% -> 0% of each run, Pallas kernels for 0% -> 0%
where the time goes in v2:
time: 335 us
  Pallas kernels  332 us (99%)
    pallas_call x1, Pallas kernels, local_mlp(): pl.pallas_call(kernel, out_shape=(jax.ShapeDtypeStruct((R, K), BF16), jax...  332 us

profile of v2, /device:TPU:0, one launch (start us, length us, event | category | flops | bytes accessed | tf_op | source)
XLA Modules:
  0.0 335.3 jit_solution(18017336118997732573)
XLA Ops:
  0.0 332.2 %mlp.1 = (bf16[1024,1024]{1,0:T(8,128)(2,1)}, bf16[4,4096,128]{2,1,0:T(8,128)(2,1)}, bf16[4,4096,256]{2,1,0:T(8,128)(2,1)}) custom-call(bf16[1024,1024]{1,0:T(8,128)(2,1)} %x.1, bf16[1024,4096]{1,0:T(8,128)(2,1)} %w1.1, bf16[8192,512]{1,0:T(8,128)(2,1)} %w2.1), custom_call_target="tpu_custom_call" | custom-call | tf_op jit(solution)/shard_map/mlp/pallas_call | solution.py:263
  332.2 3.1 copy.5

commit v3 on v0

v3 whole, which is shorter than its diff:
```python
import jax
import jax.numpy as jnp
from jax import lax
from jax.experimental import pallas as pl
from jax.experimental.pallas import tpu as pltpu
from jax.sharding import PartitionSpec as P

MESH = pl.DeviceIdType.MESH
F32, BF16 = jnp.float32, jnp.bfloat16
NE = 12
NL = 4
NA = 3
NQ = 4
MT = 512


def gelu(c):
    return c * (0.5 * (1.0 + jnp.tanh(0.7978845608028654 * (c + 0.044715 * (c * c * c)))))


def kernel(x, w1, w2, out, ap, bo, bp, co, cp, g0, eo, ep,
           xg, he, hl, w1s, w2s, w2l, zs, ry, zo, ob,
           lsem, lw, lv, lu, osem, xs, xr, ws, wr, ys, yr, zys, zyr,
           ds, dr, fs, fr):
    cz, cy, cx = lax.axis_index('cz'), lax.axis_index('cy'), lax.axis_index('cx')
    X, Y, D = {'cy': 1 - cy}, {'cz': 1 - cz}, {'cx': 1 - cx}
    R, K = x.shape
    B1 = w1.shape[1]
    WC = B1 // (NE + NL)
    EC, LC = NE * WC, NL * WC
    C2 = w2.shape[1]
    QC = 2 * C2 // NQ

    def remote(src, dst, s, r, dev):
        return pltpu.make_async_remote_copy(src, dst, s, r, device_id=dev, device_id_type=MESH)

    barrier = pltpu.get_barrier_semaphore()
    for dev in (X, Y, D):
        pl.semaphore_signal(barrier, inc=1, device_id=dev, device_id_type=MESH)
    pl.semaphore_wait(barrier, 3)

    own, oth = pl.ds(0, R), pl.ds(R, R)
    klo, khi = pl.ds(0, K), pl.ds(K, K)

    x_x = remote(x, xg.at[own, khi], xs.at[0], xr.at[0], X)
    y_x = remote(x, xg.at[oth, klo], ys.at[0], yr.at[0], Y)
    y_xf = remote(xg.at[own, khi], xg.at[oth, khi], ys.at[1], yr.at[1], Y)
    y_w1 = remote(w1.at[:, pl.ds(EC, LC)], co, ys.at[2], yr.at[2], Y)

    def y_w2(b):
        return remote(w2.at[pl.ds(b * B1 + EC, LC), :], eo.at[b], ys.at[3 + b], yr.at[3 + b], Y)

    l_x = pltpu.make_async_copy(x, xg.at[own, klo], lsem.at[0])
    d_w1 = remote(w1, ap, ds.at[0], dr.at[0], D)
    d_w2 = remote(w2, g0, ds.at[1], dr.at[1], D)
    d_co = remote(co, cp, ds.at[2], dr.at[2], D)
    d_eo = remote(eo, ep, ds.at[3], dr.at[3], D)

    def chunk(j):
        return pl.ds(j * WC if isinstance(j, int) else pl.multiple_of(j * WC, WC), WC)

    def x_w1(j):
        return remote(w1.at[:, chunk(j)], bo.at[j], ws.at[j], wr.at[j], X)

    def x_co(k):
        return remote(co.at[:, chunk(k)], bo.at[NE + NL + k], ws.at[NE + NL + k], wr.at[NE + NL + k], X)

    def f_w1(j):
        return remote(bo.at[j], bp.at[j], fs.at[j], fr.at[j], D)

    def quads(s, j, first, second):
        return [pltpu.make_async_copy(src, w1s.at[s, rows, pl.ds(c * WC, WC)], lw.at[s, i])
                for i, (src, rows, c) in enumerate((
                    (first, klo, 0), (second, klo, 1), (bo.at[j], khi, 0), (bp.at[j], khi, 1)))]

    def quads_near(s, j):
        return quads(s, j, w1.at[:, chunk(j)], ap.at[:, chunk(j)])

    def quads_far(s, k):
        return quads(s, NE + NL + k, co.at[:, chunk(k)], cp.at[:, chunk(k)])

    base = (pl.multiple_of(cx * B1, B1), pl.multiple_of((1 - cx) * B1, B1))

    def loads(q):
        src, c = (w2, q) if q < NQ // 2 else (g0, q - NQ // 2)
        return [pltpu.make_async_copy(src.at[pl.ds(base[b], EC), pl.ds(c * QC, QC)],
                                      w2s.at[q % 2, pl.ds(b * EC, EC), :], lv.at[q % 2, b]) for b in range(2)]

    def late_near(s, k):
        got = []
        for b in range(2):
            rows = pl.ds(pl.multiple_of(base[b] + EC + k * WC, WC), WC)
            for c, src in enumerate((w2, g0)):
                got.append(pltpu.make_async_copy(
                    src.at[rows, :], w2l.at[s, pl.ds(b * WC, WC), pl.ds(c * C2, C2)], lu.at[s, 2 * b + c]))
        return got

    def late_far(s, k):
        got = []
        for b, blk in enumerate((cx, 1 - cx)):
            for c, src in enumerate((eo, ep)):
                got.append(pltpu.make_async_copy(
                    src.at[blk, chunk(k), :], w2l.at[s, pl.ds(b * WC, WC), pl.ds(c * C2, C2)], lu.at[s, 2 * b + c]))
        return got

    def z_y(q):
        return remote(zs.at[q], ry.at[q], zys.at[q], zyr.at[q], Y)

    def layer1(dst, col, row0, rows, s, half):
        @pl.loop(0, rows // MT)
        def _(i):
            r = pl.multiple_of(i * MT, MT)
            c = jnp.dot(xg[pl.ds(row0 + r, MT), :], w1s[s, :, pl.ds(half * WC, WC)], preferred_element_type=F32)
            dst[pl.ds(row0 + r, MT), pl.ds(col, WC)] = gelu(c.astype(BF16).astype(F32)).astype(BF16)

    def step(j, k, near, quad, body):
        s = lax.rem(j, 2)
        q = quad(s, k)
        q[0].start()
        q[1].start()
        f = f_w1(j)
        (x_w1(j) if near else x_co(k)).wait_recv()
        f.start()
        q[2].start()
        q[0].wait()
        q[2].wait()
        body(s, 0)
        f.wait_recv()
        q[3].start()
        q[1].wait()
        q[3].wait()
        body(s, 1)

    x_x.start()
    y_x.start()
    l_x.start()
    for j in range(NE):
        x_w1(j).start()
    d_w1.start()
    d_w2.start()
    for q in range(2):
        for c in loads(q):
            c.start()

    x_x.wait_recv()
    y_xf.start()
    y_w1.start()
    y_w2(0).start()
    y_w2(1).start()
    l_x.wait()
    d_w1.wait_recv()

    def col(j, half):
        return pl.multiple_of(half * EC + j * WC, WC)

    @pl.loop(0, NA)
    def _(j):
        step(j, j, True, quads_near, lambda s, half: layer1(he, col(j, half), 0, R, s, half))

    y_x.wait_recv()
    y_xf.wait_recv()

    @pl.loop(0, NA)
    def _(j):
        s = lax.rem(j, 2)
        for c in quads_near(s, j):
            c.start()
        for c in quads_near(s, j):
            c.wait()
        for half in range(2):
            layer1(he, col(j, half), R, R, s, half)

    def early(lo, hi):
        @pl.loop(lo, hi)
        def _(j):
            step(j, j, True, quads_near, lambda s, half: layer1(he, col(j, half), 0, 2 * R, s, half))

    early(NA, 8)
    y_w1.wait_recv()
    for k in range(NL):
        x_w1(NE + k).start()
    for k in range(NL):
        x_co(k).start()
    d_co.start()
    y_w2(0).wait_recv()
    y_w2(1).wait_recv()
    d_eo.start()
    early(8, NE)

    d_w2.wait_recv()
    for q in range(NQ):
        for c in loads(q):
            c.wait()

        @pl.loop(0, R // MT)
        def _(i):
            r = pl.multiple_of(i * MT, MT)
            zs[q, pl.ds(r, MT), :] = jnp.dot(he[pl.ds(R + r, MT), :], w2s[q % 2], preferred_element_type=F32)

        z_y(q).start()

        @pl.loop(0, R // MT)
        def _(i):
            r = pl.multiple_of(i * MT, MT)
            zo[pl.ds(r, MT), pl.ds(q * QC, QC)] = jnp.dot(he[pl.ds(r, MT), :], w2s[q % 2], preferred_element_type=F32)

        if q + 2 < NQ:
            for c in loads(q + 2):
                c.start()

    d_co.wait_recv()
    d_eo.wait_recv()

    def late(near):
        off = NE if near else NE + NL
        quad = quads_near if near else quads_far
        lo = NE if near else 0

        @pl.loop(0, NL)
        def _(k):
            s = lax.rem(off + k, 2)
            lw2 = late_near(s, k) if near else late_far(s, k)
            for c in lw2:
                c.start()
            step(off + k, lo + k, near, quad, lambda s, half: layer1(hl, half * WC, 0, R, s, half))
            for c in lw2:
                c.wait()

            @pl.loop(0, R // MT)
            def _(i):
                r = pl.ds(pl.multiple_of(i * MT, MT), MT)
                zo[r, :] = zo[r, :] + jnp.dot(hl[r, :], w2l[s], preferred_element_type=F32)

    late(True)
    late(False)

    def store(q):
        half, c = divmod(q, NQ // 2)
        lanes = pl.multiple_of((1 - cx if half else cx) * C2 + c * QC, QC)
        return pltpu.make_async_copy(ob.at[:, pl.ds(q * QC, QC)], out.at[:, pl.ds(lanes, QC)], osem.at[q])

    for q in range(NQ):
        z_y(q).wait_recv()
        ob[:, pl.ds(q * QC, QC)] = (zo[:, pl.ds(q * QC, QC)] + ry[q]).astype(BF16)
        store(q).start()
    for q in range(NQ):
        z_y(q).wait_send()
        store(q).wait()
    for c in [x_x, y_x, y_xf, y_w1, y_w2(0), y_w2(1), d_w1, d_w2, d_co, d_eo]:
        c.wait_send()

    @pl.loop(0, NE + NL)
    def _(j):
        x_w1(j).wait_send()

    @pl.loop(0, NL)
    def _(k):
        x_co(k).wait_send()

    @pl.loop(0, NE + 2 * NL)
    def _(j):
        f_w1(j).wait_send()


def solution(mesh):
    data_spec = P(('dp', 'cx', 'cz'), 'cy')
    up_spec = P('cy', ('cz', 'cx'))
    down_spec = P('cz', ('cy', 'cx'))

    def local_mlp(x, w1, w2):
        R, K = x.shape
        B1 = w1.shape[1]
        WC = B1 // (NE + NL)
        EC, LC = NE * WC, NL * WC
        C2 = w2.shape[1]
        QC = 2 * C2 // NQ
        NX = NE + 2 * NL
        dma = pltpu.SemaphoreType.DMA
        any_spec = pl.BlockSpec(memory_space=pl.ANY)
        sds = jax.ShapeDtypeStruct
        outs = (
            sds((R, K), BF16),
            sds(w1.shape, BF16),
            sds((NX, K, WC), BF16),
            sds((NX, K, WC), BF16),
            sds((K, LC), BF16),
            sds((K, LC), BF16),
            sds(w2.shape, BF16),
            sds((2, LC, C2), BF16),
            sds((2, LC, C2), BF16),
        )
        scratch = [
            pltpu.VMEM((2 * R, 2 * K), BF16),
            pltpu.VMEM((2 * R, 2 * EC), BF16),
            pltpu.VMEM((R, 2 * WC), BF16),
            pltpu.VMEM((2, 2 * K, 2 * WC), BF16),
            pltpu.VMEM((2, 2 * EC, QC), BF16),
            pltpu.VMEM((2, 2 * WC, 2 * C2), BF16),
            pltpu.VMEM((NQ, R, QC), F32),
            pltpu.VMEM((NQ, R, QC), F32),
            pltpu.VMEM((R, 2 * C2), F32),
            pltpu.VMEM((R, 2 * C2), BF16),
            dma((1,)), dma((2, 4)), dma((2, 2)), dma((2, 4)), dma((NQ,)),
            dma((1,)), dma((1,)),
            dma((NX,)), dma((NX,)),
            dma((5,)), dma((5,)),
            dma((NQ,)), dma((NQ,)),
            dma((4,)), dma((4,)),
            dma((NX,)), dma((NX,)),
        ]
        return pl.pallas_call(
            kernel,
            out_shape=outs,
            in_specs=[any_spec] * 3,
            out_specs=(any_spec,) * len(outs),
            scratch_shapes=scratch,
            compiler_params=pltpu.CompilerParams(
                collective_id=0, has_side_effects=True, vmem_limit_bytes=67043328),
            name='mlp',
        )(x, w1, w2)[0]

    return jax.shard_map(local_mlp, mesh=mesh, in_specs=(data_spec, up_spec, down_spec), out_specs=data_spec, check_vma=False)
```

time: 1440 us -> 324 us (0.23)
  waiting for transfers between devices: 1310 us -> 0 us
  Pallas kernels: 0 us -> 319 us
  matrix products: 88.2 us -> 0 us
  other arithmetic: 24.9 us -> 0 us
    reduce_scatter x2 -> x0, waiting for transfers between devices: 823 us -> none  [the longest x1 726 us: local_mlp(): lax.psum_scatter(partial_up, 'cy', scatter_dimension=0, tiled=True)]
    all_gather x4 -> x0, waiting for transfers between devices: 483 us -> none  [the longest x1 388 us: local_mlp(): hidden_block = lax.all_gather(hidden, 'cy', axis=0, tiled=True)]
    pallas_call x0 -> x1, Pallas kernels: none -> 319 us  [local_mlp(): pl.pallas_call(kernel, out_shape=outs, in_specs=[any_spec] * 3, out_specs...]
    dot_general x2 -> x0, matrix products: 88.2 us -> none  [the longest x1 44.8 us: local_mlp(): jnp.dot(x_block, w_up_block, preferred_element_type=jnp.float32)]
    convert_element_type x2 -> x0, other arithmetic: 24.9 us -> none  [the longest x1 21.1 us: local_mlp(): jax.nn.gelu(pre_act.astype(jnp.bfloat16).astype(jnp.float32), approximate...]
  transfers between devices with their start and end apart: 6 -> 0, of which waited for: 6 -> 0; matrix products, arithmetic and copies ran while one was open for 1% -> 0% of each run, Pallas kernels for 0% -> 0%
where the time goes in v3:
time: 324 us; the launch traced here: 322 us
  Pallas kernels  319 us (98%)
    pallas_call x1, Pallas kernels, local_mlp(): pl.pallas_call(kernel, out_shape=outs, in_specs=[any_spec] * 3, out_specs...  319 us

profile of v3, /device:TPU:0, one launch (start us, length us, event | category | flops | bytes accessed | tf_op | source)
XLA Modules:
  0.0 322.1 jit_solution(3681756485563491117)
XLA Ops:
  0.0 319.1 %mlp.1 = (bf16[1024,1024]{1,0:T(8,128)(2,1)}, bf16[1024,4096]{1,0:T(8,128)(2,1)}, bf16[20,1024,256]{2,1,0:T(8,128)(2,1)}, bf16[20,1024,256]{2,1,0:T(8,128)(2,1)}...) custom-call(bf16[1024,1024]{1,0:T(8,128)(2,1)} %x.1, ...), custom_call_target="tpu_custom_call" | custom-call | tf_op jit(solution)/shard_map/mlp/pallas_call | solution.py:311
  319.1 3.1 copy.5
